TPU v7x, 512 devices: a whole 4x4x16 slice. The times are simulated.
512 devices in a mesh: uly: 8 (over y, core), blk: 64 (over x, z).
Axes of the slice: x: 4, y: 4, z: 16, core: 2. Of those that a mesh axis runs over, the one named last changes fastest.
Arguments:
- query_inputs: bfloat16 [65536, 2048], P(('blk', 'uly')), may hold values from -6 to 6
- key_inputs: bfloat16 [65536, 1024], P(('blk', 'uly')), may hold values from -6 to 6
- value_inputs: bfloat16 [65536, 1024], P(('blk', 'uly')), may hold values from -6 to 6
- forward_out: bfloat16 [65536, 2048], P(('blk', 'uly')), may hold values from -6 to 6
- output_gradient: bfloat16 [65536, 2048], P(('blk', 'uly')), may hold values from -4 to 4
- lse_parts: float32 [65536, 16, 2], P(('blk', 'uly')), may hold values from 3 to 247
- segment_ids: int32 [65536], P(('blk', 'uly')), may hold values from 0 to 127, never falling along the last dimension, each value on 1 to 2048 neighbouring positions
Outputs:
- query_grad: bfloat16 [65536, 2048], P(('blk', 'uly'))
- key_grad: bfloat16 [65536, 1024], P(('blk', 'uly'))
- value_grad: bfloat16 [65536, 1024], P(('blk', 'uly'))
Inputs may be any that keep to these rules, and one draw needn't show every extreme that they name: `segment_ids`: never falls along the sequence; every document holds 1 to 2048 tokens, and some document exactly 2048.
All inputs are finite; a program needn't handle non-finite values.
Results may differ from a plain program's by a relative error of at most 0.0051.
Values may be sent and summed in bfloat16 or wider, within the bound.
A program may use at most 128 MiB of HBM per device.

v0:
```python
import functools
import math

import jax
import jax.numpy as jnp
from jax import lax
from jax.experimental import pallas as pl
from jax.experimental.pallas import tpu as pltpu
from jax.sharding import PartitionSpec as P

HEAD_SIZE = 128
QUERY_HEADS = 16
KEY_VALUE_HEADS = 8
GROUP = QUERY_HEADS // KEY_VALUE_HEADS
TILE = 256
PIECES = 2
FAR = -1e30


def dot_nt(a, b):
    return lax.dot_general(a, b, (((1,), (1,)), ((), ())), preferred_element_type=jnp.float32)


def dot_nn(a, b):
    return lax.dot_general(a, b, (((1,), (0,)), ((), ())), preferred_element_type=jnp.float32)


def dot_tn(a, b):
    return lax.dot_general(a, b, (((0,), (0,)), ((), ())), preferred_element_type=jnp.float32)


def kernel(
    uly_count, blk_count,
    q_ref, do_hbm, k_hbm, v_hbm, out_hbm, lp_hbm, ids_hbm,
    dq_ref, dk_ref, dv_ref,
    qb, dob, kvb, statb, idb, bias,
    dqacc, acc0, acc2, dqs, ret1, ret2, in1, in2, dkvs,
    do_ref, k_ref, v_ref, out_ref, lp_ref, ids_ref, stat_ref,
    loc_sem, keep_sem,
    kv_s, kv_r, qd_s, qd_r, st_s, st_r, id_s, id_r,
    h2_s, h2_r, h2i_s, h2i_r, pt_s, pt_r, pti_s, pti_r,
    r1_s, r1_r, r2_s, r2_r, oq_s, oq_r, okv_s, okv_r,
):
    U, B = uly_count, blk_count
    T = q_ref.shape[0]
    R = T * U
    KH = KEY_VALUE_HEADS // U
    D = HEAD_SIZE
    GD = GROUP * D
    scale = 1.0 / math.sqrt(D)
    u = lax.axis_index("uly")
    b = lax.axis_index("blk")
    odd = lax.rem(b, 2)
    even = odd == 0
    mate = b + 1 - 2 * odd

    def at(blk, uly):
        return {"blk": blk, "uly": uly}

    def rcopy(src, dst, ssem, rsem, dev):
        return pltpu.make_async_remote_copy(
            src_ref=src, dst_ref=dst, send_sem=ssem, recv_sem=rsem,
            device_id=dev, device_id_type=pl.DeviceIdType.MESH,
        )

    def cols(first, width):
        return pl.ds(pl.multiple_of(first, 128), width)

    def rows(place):
        return pl.ds(pl.multiple_of(place * T, T), T)

    has_up2 = b + 2 < B
    has_down2 = b >= 2
    sends_mate = jnp.logical_or(even, b >= 3)

    loads = [
        pltpu.make_async_copy(src, dst, loc_sem.at[5 + i])
        for i, (src, dst) in enumerate([
            (ids_hbm, ids_ref), (k_hbm, k_ref), (v_hbm, v_ref),
            (do_hbm, do_ref), (out_hbm, out_ref), (lp_hbm, lp_ref),
        ])
    ]
    own_kv = [
        pltpu.make_async_copy(
            k_hbm.at[:, cols(u * KH * D, KH * D)], kvb.at[0, 0, rows(u), :], loc_sem.at[2]
        ),
        pltpu.make_async_copy(
            v_hbm.at[:, cols(u * KH * D, KH * D)], kvb.at[0, 1, rows(u), :], loc_sem.at[3]
        ),
    ]
    for copy in own_kv + loads:
        copy.start()

    barrier = pltpu.get_barrier_semaphore()
    for k in range(1, U):
        pl.semaphore_signal(
            barrier, inc=1, device_id=at(b, lax.rem(u + k, U)), device_id_type=pl.DeviceIdType.MESH
        )
    pl.semaphore_signal(barrier, inc=1, device_id=at(mate, u), device_id_type=pl.DeviceIdType.MESH)

    @pl.when(has_up2)
    def _():
        pl.semaphore_signal(
            barrier, inc=1, device_id=at(b + 2, u), device_id_type=pl.DeviceIdType.MESH
        )

    @pl.when(has_down2)
    def _():
        pl.semaphore_signal(
            barrier, inc=1, device_id=at(b - 2, u), device_id_type=pl.DeviceIdType.MESH
        )

    expected = U + has_up2.astype(jnp.int32) + has_down2.astype(jnp.int32)
    pl.semaphore_wait(barrier, expected)

    own_q = [
        pltpu.make_async_copy(
            q_ref.at[:, cols(u * KH * GD, KH * GD)], qb.at[rows(u), :], loc_sem.at[0]
        ),
        pltpu.make_async_copy(
            do_hbm.at[:, cols(u * KH * GD, KH * GD)], dob.at[rows(u), :], loc_sem.at[1]
        ),
    ]
    own_id = pltpu.make_async_copy(ids_hbm, idb.at[0, u], loc_sem.at[4])

    def id_in(k, place, dev):
        return rcopy(ids_ref, idb.at[0, place], id_s.at[k - 1], id_r.at[k - 1], dev)

    def st_in(k, place, peer, dev):
        return rcopy(stat_ref.at[peer], statb.at[place], st_s.at[k - 1], st_r.at[k - 1], dev)

    def kv_in(k, which, j, place, peer, dev):
        ref = (k_ref, v_ref)[which]
        return rcopy(
            ref.at[:, cols((peer * KH + j) * D, D)],
            kvb.at[0, which, rows(place), cols(j * D, D)],
            kv_s.at[which, j, k - 1], kv_r.at[which, j, k - 1], dev,
        )

    def qd_in(k, which, j, place, peer, dev):
        ref, buf = ((q_ref, qb), (do_ref, dob))[which]
        return rcopy(
            ref.at[:, cols((peer * KH + j) * GD, GD)],
            buf.at[rows(place), cols(j * GD, GD)],
            qd_s.at[which, j, k - 1], qd_r.at[which, j, k - 1], dev,
        )

    def h2(j, i, place):
        return rcopy(
            kvb.at[0, :, rows(place), cols(j * D, D)], kvb.at[2, :, rows(place), cols(j * D, D)],
            h2_s.at[j, i], h2_r.at[j, i], at(b + 2, u),
        )

    peers = [(k, lax.rem(u + k, U), lax.rem(u + U - k, U)) for k in range(1, U)]
    shares = [(0, u)] + [(k, frm) for k, _, frm in peers]
    for copy in own_kv:
        copy.wait()

    @pl.when(has_up2)
    def _():
        for j in range(KH):
            h2(j, 0, u).start()

    loads[0].wait()
    for k, to, _ in peers:
        id_in(k, u, at(b, to)).start()
    loads[1].wait()
    loads[2].wait()
    for j in range(KH):
        for k, to, _ in peers:
            for which in range(2):
                kv_in(k, which, j, u, to, at(b, to)).start()
    for copy in [own_id] + own_q:
        copy.start()

    for copy in loads[3:]:
        copy.wait()
    G = KH * GROUP
    lane = lax.broadcasted_iota(jnp.int32, (T, 128), 1)
    table = jnp.zeros((T, 128), jnp.float32)
    for h in range(U * G):
        piece = slice(h * D, (h + 1) * D)
        total = jnp.sum(
            do_ref[:, piece].astype(jnp.float32) * out_ref[:, piece].astype(jnp.float32),
            axis=1, keepdims=True,
        )
        table = jnp.where(lane == h, total, table)
    table = table.T
    part0, part1 = lp_ref[:, 0, :], lp_ref[:, 1, :]
    highest = jnp.maximum(part0, part1)
    lse_rows = highest + jnp.log(jnp.exp(part0 - highest) + jnp.exp(part1 - highest))
    for p in range(U):
        stat_ref[p, :G, :] = lse_rows[p * G:(p + 1) * G]
        stat_ref[p, G:2 * G, :] = table[p * G:(p + 1) * G]
    statb[u] = stat_ref[u]

    for j in range(KH):
        for k, to, _ in peers:
            for which in range(2):
                qd_in(k, which, j, u, to, at(b, to)).start()
        if j == 0:
            for k, to, _ in peers:
                st_in(k, u, to, at(b, to)).start()


    def h2id():
        return rcopy(idb.at[0], idb.at[2], h2i_s.at[0], h2i_r.at[0], at(b + 2, u))

    def pt(j):
        return rcopy(
            kvb.at[2 * odd, :, :, cols(j * D, D)], kvb.at[1, :, :, cols(j * D, D)],
            pt_s.at[j], pt_r.at[j], at(mate, u),
        )

    def ptid():
        return rcopy(idb.at[2 * odd], idb.at[1], pti_s.at[0], pti_r.at[0], at(mate, u))

    own_id.wait()
    for k, _, frm in peers:
        id_in(k, frm, at(b, frm)).wait_recv()

    @pl.when(has_up2)
    def _():
        h2id().start()

    @pl.when(even)
    def _():
        ptid().start()

    for j in range(KH):
        for k, _, frm in peers:
            for which in range(2):
                kv_in(k, which, j, frm, frm, at(b, frm)).wait_recv()

        @pl.when(has_up2)
        def _():
            for k, _, frm in peers:
                h2(j, k, frm).start()

        @pl.when(even)
        def _():
            pt(j).start()

    def make_bias(hop):
        for kp in range(U):
            key_ids = jnp.broadcast_to(idb[hop, kp, 0:1, :].astype(jnp.float32), (T, T)).T
            for qp in range(U):
                query_ids = idb[0, qp, 0:1, :].astype(jnp.float32)
                good = key_ids == query_ids
                if hop == 0:
                    kpos = lax.broadcasted_iota(jnp.int32, (T, T), 0) + kp * T
                    qpos = lax.broadcasted_iota(jnp.int32, (T, T), 1) + qp * T
                    good = jnp.logical_and(good, kpos <= qpos)
                bias[hop, kp * T:(kp + 1) * T, qp * T:(qp + 1) * T] = jnp.where(good, 0.0, FAR)

    make_bias(0)

    @pl.when(has_down2)
    def _():
        h2id().wait_recv()
        make_bias(2)

        @pl.when(odd == 1)
        def _():
            ptid().start()

    def arrive2(j):
        @pl.when(has_down2)
        def _():
            for i, place in shares:
                h2(j, i, place).wait_recv()

            @pl.when(odd == 1)
            def _():
                pt(j).start()

    arrive2(0)

    @pl.when(b >= 1)
    def _():
        ptid().wait_recv()
        make_bias(1)

    for copy in own_q:
        copy.wait()
    for k, _, frm in peers:
        st_in(k, frm, frm, at(b, frm)).wait_recv()

    tile = min(TILE, R)
    steps = R // tile
    per = tile // T if tile >= T else 1

    def stat_row(row, qt):
        parts = [statb[qt * per + i, pl.ds(row, 1), :] for i in range(per)]
        return parts[0] if per == 1 else jnp.concatenate(parts, axis=1)

    def hop_grads(hop, j, acc):
        def key_step(kt, _):
            krow = pl.ds(pl.multiple_of(kt * tile, tile), tile)
            kc = kvb[hop, 0, krow, cols(j * D, D)]
            vc = kvb[hop, 1, krow, cols(j * D, D)]

            def query_step(qt, carry):
                dk, dv = carry
                qrow = pl.ds(pl.multiple_of(qt * tile, tile), tile)
                for g in range(GROUP):
                    qc = qb[qrow, cols(j * GD + g * D, D)]
                    dc = dob[qrow, cols(j * GD + g * D, D)]
                    head = j * GROUP + g
                    lse = stat_row(head, qt)
                    delta = stat_row(G + head, qt)
                    w = jnp.exp(dot_nt(kc, qc) * scale - lse + bias[hop, krow, pl.ds(pl.multiple_of(qt * tile, tile), tile)])
                    dv = dv + dot_nn(w.astype(jnp.bfloat16), dc)
                    ds = (w * (dot_nt(vc, dc) - delta)).astype(jnp.bfloat16)
                    dk = dk + dot_nn(ds, qc)
                    part = dot_tn(ds, kc)
                    dqacc[qrow, g * D:(g + 1) * D] += part
                return dk, dv

            zero = jnp.zeros((tile, D), jnp.float32)
            if steps == 1:
                dk, dv = query_step(0, (zero, zero))
            else:
                dk, dv = lax.fori_loop(0, steps, query_step, (zero, zero))
            acc[j, 0, krow, :] = (dk * scale).astype(acc.dtype)
            acc[j, 1, krow, :] = dv.astype(acc.dtype)
            return 0

        if steps == 1:
            key_step(0, 0)
        else:
            lax.fori_loop(0, steps, key_step, 0)

    def give1(j):
        return rcopy(ret1.at[j], in1.at[j], r1_s.at[j], r1_r.at[j], at(mate, u))

    def give2(j):
        return rcopy(ret2.at[j], in2.at[j], r2_s.at[j], r2_r.at[j], at(b - 2, u))

    def oq(k, j, place, dev):
        return rcopy(
            dqs.at[j, rows(place), :], dq_ref.at[:, cols((u * KH + j) * GD, GD)],
            oq_s.at[j, k - 1], oq_r.at[j, k - 1], dev,
        )

    def okv(k, which, j, place, dev):
        ref = (dk_ref, dv_ref)[which]
        return rcopy(
            dkvs.at[j, which, rows(place), :], ref.at[:, cols((u * KH + j) * D, D)],
            okv_s.at[which, j, k - 1], okv_r.at[which, j, k - 1], dev,
        )

    def keep_q(j):
        return pltpu.make_async_copy(
            dqs.at[j, rows(u), :], dq_ref.at[:, cols((u * KH + j) * GD, GD)], keep_sem.at[2, j]
        )

    def keep_kv(which, j):
        ref = (dk_ref, dv_ref)[which]
        return pltpu.make_async_copy(
            dkvs.at[j, which, rows(u), :], ref.at[:, cols((u * KH + j) * D, D)],
            keep_sem.at[which, j],
        )

    def compute(j):
        for k, _, frm in peers:
            for which in range(2):
                qd_in(k, which, j, frm, frm, at(b, frm)).wait_recv()
        dqacc[...] = jnp.zeros_like(dqacc)

        @pl.when(b >= 1)
        def _():
            pt(j).wait_recv()
            hop_grads(1, j, ret1)
            give1(j).start()

        @pl.when(has_down2)
        def _():
            hop_grads(2, j, acc2)

        stage_a(j)
        hop_grads(0, j, acc0)

        dqs[j] = (dqacc[...] * scale).astype(jnp.bfloat16)
        for k, to, _ in peers:
            oq(k, j, to, at(b, to)).start()
        keep_q(j).start()

    def stage_a(j):
        @pl.when(jnp.logical_and(odd == 1, has_down2))
        def _():
            give1(j).wait_recv()
            ret2[j] = (acc2[j] + in1[j].astype(jnp.float32)).astype(jnp.bfloat16)

        @pl.when(jnp.logical_and(even, has_down2))
        def _():
            ret2[j] = acc2[j].astype(jnp.bfloat16)

        @pl.when(has_down2)
        def _():
            give2(j).start()

    def stage_b(j):
        @pl.when(even)
        def _():
            give1(j).wait_recv()
            acc0[j] += in1[j].astype(jnp.float32)

        @pl.when(has_up2)
        def _():
            give2(j).wait_recv()
            acc0[j] += in2[j].astype(jnp.float32)

        dkvs[j] = acc0[j].astype(jnp.bfloat16)
        for k, to, _ in peers:
            for which in range(2):
                okv(k, which, j, to, at(b, to)).start()
        for which in range(2):
            keep_kv(which, j).start()

    def head_step(j, _):
        @pl.when(j + 1 < KH)
        def _():
            arrive2(jnp.minimum(j + 1, KH - 1))

        compute(j)

        @pl.when(j >= 2)
        def _():
            stage_b(jnp.maximum(j - 2, 0))

        return 0

    lax.fori_loop(0, KH, head_step, 0)
    if KH >= 2:
        stage_b(KH - 2)
    stage_b(KH - 1)

    for k, to, frm in peers:
        id_in(k, u, at(b, to)).wait_send()
        st_in(k, u, to, at(b, to)).wait_send()

    @pl.when(has_up2)
    def _():
        h2id().wait_send()

    @pl.when(sends_mate)
    def _():
        ptid().wait_send()

    def finish(j, _):
        keep_q(j).wait()
        for which in range(2):
            keep_kv(which, j).wait()
        for k, to, frm in peers:
            for which in range(2):
                kv_in(k, which, j, u, to, at(b, to)).wait_send()
                qd_in(k, which, j, u, to, at(b, to)).wait_send()

        @pl.when(has_up2)
        def _():
            for i, place in shares:
                h2(j, i, place).wait_send()

        @pl.when(sends_mate)
        def _():
            pt(j).wait_send()

        @pl.when(b >= 1)
        def _():
            give1(j).wait_send()

        @pl.when(has_down2)
        def _():
            give2(j).wait_send()

        for k, to, frm in peers:
            oq(k, j, to, at(b, to)).wait_send()
            for which in range(2):
                okv(k, which, j, to, at(b, to)).wait_send()
            rcopy(
                dqs.at[j, rows(frm), :], dq_ref.at[:, cols((frm * KH + j) * GD, GD)],
                oq_s.at[j, k - 1], oq_r.at[j, k - 1], at(b, frm),
            ).wait_recv()
            for which in range(2):
                ref = (dk_ref, dv_ref)[which]
                rcopy(
                    dkvs.at[j, which, rows(frm), :], ref.at[:, cols((frm * KH + j) * D, D)],
                    okv_s.at[which, j, k - 1], okv_r.at[which, j, k - 1], at(b, frm),
                ).wait_recv()
        return 0

    lax.fori_loop(0, KH, finish, 0)


def close_kernel(a_in, b_in, c_in, a_out, b_out, c_out, a_mid, b_mid, c_mid, in_sem, out_sem):
    moves = []
    for i, (src, mid, dst) in enumerate(
        [(a_in, a_mid, a_out), (b_in, b_mid, b_out), (c_in, c_mid, c_out)]
    ):
        height = src.shape[0] // PIECES
        for n in range(PIECES):
            part = pl.ds(n * height, height)
            moves.append((
                pltpu.make_async_copy(src.at[part], mid.at[part], in_sem.at[i, n]),
                pltpu.make_async_copy(mid.at[part], dst.at[part], out_sem.at[i, n]),
            ))
    for load, _ in moves:
        load.start()
    for load, store in moves:
        load.wait()
        store.start()
    for _, store in moves:
        store.wait()


def per_device(uly_count, blk_count, q, k, v, out, grad, lse_parts, segment_ids):
    U, B = uly_count, blk_count
    T = q.shape[0]
    R = T * U
    KH = KEY_VALUE_HEADS // U
    G = KH * GROUP
    D = HEAD_SIZE
    stat_rows = -(-2 * G // 8) * 8
    parts = lse_parts.transpose(1, 2, 0)
    ids = segment_ids.reshape(1, T)
    bf, f32 = jnp.bfloat16, jnp.float32
    n = max(U - 1, 1)
    dma = pltpu.SemaphoreType.DMA
    sems = []
    for shape in [(2, KH, n), (2, KH, n), (n,), (n,), (KH, U), (1,), (KH,), (1,), (KH,), (KH,), (KH, n), (2, KH, n)]:
        sems += [dma(shape), dma(shape)]
    vm = pltpu.VMEM
    results = pl.pallas_call(
        functools.partial(kernel, U, B),
        out_shape=(
            jax.ShapeDtypeStruct(q.shape, bf),
            jax.ShapeDtypeStruct(k.shape, bf),
            jax.ShapeDtypeStruct(v.shape, bf),
        ),
        in_specs=[pl.BlockSpec(memory_space=pltpu.HBM)] * 7,
        out_specs=tuple([pl.BlockSpec(memory_space=pltpu.HBM)] * 3),
        scratch_shapes=[
            vm((R, G * D), bf),
            vm((R, G * D), bf),
            vm((3, 2, R, KH * D), bf),
            vm((U, stat_rows, T), f32),
            vm((3, U, 1, T), jnp.int32),
            vm((3, R, R), f32),
            vm((R, GROUP * D), f32),
            vm((KH, 2, R, D), f32),
            vm((KH, 2, R, D), f32),
            vm((KH, R, GROUP * D), bf),
            vm((KH, 2, R, D), bf),
            vm((KH, 2, R, D), bf),
            vm((KH, 2, R, D), bf),
            vm((KH, 2, R, D), bf),
            vm((KH, 2, R, D), bf),
            vm(q.shape, bf),
            vm(k.shape, bf),
            vm(v.shape, bf),
            vm(q.shape, bf),
            vm(parts.shape, f32),
            vm((1, T), jnp.int32),
            vm((U, stat_rows, T), f32),
            dma((11,)),
            dma((3, KH)),
        ] + sems,
        compiler_params=pltpu.CompilerParams(
            collective_id=0, has_side_effects=True, vmem_limit_bytes=56 << 20
        ),
    )(q, grad, k, v, out, parts, ids)
    hbm = [pl.BlockSpec(memory_space=pltpu.HBM)] * 3
    return pl.pallas_call(
        close_kernel,
        out_shape=tuple(jax.ShapeDtypeStruct(r.shape, r.dtype) for r in results),
        in_specs=hbm,
        out_specs=tuple(hbm),
        scratch_shapes=[vm(r.shape, r.dtype) for r in results]
        + [dma((3, PIECES)), dma((3, PIECES))],
        compiler_params=pltpu.CompilerParams(vmem_limit_bytes=56 << 20),
    )(*results)


def solution(mesh):
    spec = P(("blk", "uly"), None)
    body = functools.partial(per_device, mesh.shape["uly"], mesh.shape["blk"])
    return jax.shard_map(
        body,
        mesh=mesh,
        in_specs=(spec, spec, spec, spec, spec, P(("blk", "uly"), None, None), P(("blk", "uly"))),
        out_specs=(spec, spec, spec),
        check_vma=False,
    )
```

profile of v0, /device:TPU:7, one launch (start us, length us, event | category | flops | bytes accessed | tf_op | source)
XLA Modules:
  0.0 119.1 jit_solution(11369957257073140395)
XLA Ops:
  0.6 116.5 %shard_map.94 = (bf16[128,2048]{1,0:T(8,128)(2,1)}, bf16[128,1024]{1,0:T(8,128)(2,1)}, bf16[128,1024]{1,0:T(8,128)(2,1)}) custom-call(bf16[128,2048]{1,0:T(8,128)(2,1)} %q_ref.1, bf16[128,2048]{1,0:T(8,128)(2,1)} %do_hbm.1, bf16[128,1024]{1,0:T(8,128)(2,1)} %k_hbm.1, bf16[128,1024]{1,0:T(8,128)(2,1)} %v_hbm.1, bf16[128,2048]{1,0:T(8,128)(2,1)} %out_hbm.1, ...), custom_call_target="tpu_custom_call" | custom-call | tf_op jit(solution)/shard_map/pallas_call | solution.py:534
  117.1 2.0 %shard_map.95 = (bf16[128,2048]{1,0:T(8,128)(2,1)}, bf16[128,1024]{1,0:T(8,128)(2,1)}, bf16[128,1024]{1,0:T(8,128)(2,1)}) custom-call(bf16[128,2048]{1,0:T(8,128)(2,1)} %get-tuple-element.6.a_in, bf16[128,1024]{1,0:T(8,128)(2,1)} %get-tuple-element.7.b_in, bf16[128,1024]{1,0:T(8,128)(2,1)} %get-tuple-element.8.c_in), custom_call_target="tpu_custom_call" | custom-call | tf_op jit(solution)/shard_map/pallas_call | solution.py:574
where the time goes:
time: 119 us
  Pallas kernels  118 us (99%)
    pallas_call x1, Pallas kernels, per_device(): pl.pallas_call(functools.partial(kernel, U, B), out_shape=(jax.ShapeDtype...  116 us

commit v1 on v0

v1 whole, which is shorter than its diff:
```python
import functools
import math

import jax
import jax.numpy as jnp
from jax import lax
from jax.experimental import pallas as pl
from jax.experimental.pallas import tpu as pltpu
from jax.sharding import PartitionSpec as P

HEAD_SIZE = 128
QUERY_HEADS = 16
KEY_VALUE_HEADS = 8
GROUP = QUERY_HEADS // KEY_VALUE_HEADS
PIECES = 2
FAR = 8192.0


def dot(a, b):
    return lax.dot_general(a, b, (((1,), (0,)), ((), ())), preferred_element_type=jnp.float32)


def kernel(
    uly_count, blk_count,
    q_hbm, do_hbm, k_hbm, v_hbm, out_hbm, lp_hbm, ids_hbm,
    dq_ref, dk_ref, dv_ref,
    q_in, do_in, k_in, v_in, out_in, lp_in, ids_in,
    qb, dob, kvb, stat_ref, statb,
    aug, kaug, vaug, qT, dT, kT, vT,
    dqa, dka, dva,
    retk, retq, ink, inq, dqs, dkvs,
    loc_sem, keep_sem,
    qd_s, qd_r, kv_s, kv_r, st_s, st_r,
    zq_s, zq_r, zk_s, zk_r, zst_s, zst_r,
    rk_s, rk_r, rq_s, rq_r, oq_s, oq_r, okv_s, okv_r,
):
    U, B = uly_count, blk_count
    T = q_hbm.shape[0]
    R = T * U
    D = HEAD_SIZE
    GD = GROUP * D
    H = R // 2
    bf, f32 = jnp.bfloat16, jnp.float32
    scale = 1.0 / math.sqrt(D)
    u = lax.axis_index("uly")
    b = lax.axis_index("blk")
    has_dn = b >= 1
    has_up = b + 1 < B
    mid = jnp.logical_and(has_dn, has_up)

    def at(blk, uly):
        return {"blk": blk, "uly": uly}

    def rcopy(src, dst, ssem, rsem, dev):
        return pltpu.make_async_remote_copy(
            src_ref=src, dst_ref=dst, send_sem=ssem, recv_sem=rsem,
            device_id=dev, device_id_type=pl.DeviceIdType.MESH,
        )

    def cols(first, width):
        return pl.ds(pl.multiple_of(first, 128), width)

    def rows(place, base=0):
        return pl.ds(pl.multiple_of(base + place * T, T), T)

    def each(low, high, step):
        def body(i, c):
            step(i)
            return c
        lax.fori_loop(low, high, body, 0)

    barrier = pltpu.get_barrier_semaphore()
    for k in range(1, U):
        pl.semaphore_signal(
            barrier, inc=1, device_id=at(b, lax.rem(u + k, U)), device_id_type=pl.DeviceIdType.MESH
        )

    @pl.when(has_up)
    def _():
        pl.semaphore_signal(barrier, inc=1, device_id=at(b + 1, u), device_id_type=pl.DeviceIdType.MESH)

    @pl.when(has_dn)
    def _():
        pl.semaphore_signal(barrier, inc=1, device_id=at(b - 1, u), device_id_type=pl.DeviceIdType.MESH)

    loads = [
        pltpu.make_async_copy(src, dst, loc_sem.at[i])
        for i, (src, dst) in enumerate([
            (q_hbm, q_in), (do_hbm, do_in), (k_hbm, k_in), (v_hbm, v_in),
            (out_hbm, out_in), (lp_hbm, lp_in), (ids_hbm, ids_in),
        ])
    ]
    own = [
        pltpu.make_async_copy(q_hbm.at[:, cols(u * GD, GD)], qb.at[rows(u), :], loc_sem.at[7]),
        pltpu.make_async_copy(do_hbm.at[:, cols(u * GD, GD)], dob.at[rows(u), :], loc_sem.at[8]),
        pltpu.make_async_copy(k_hbm.at[:, cols(u * D, D)], kvb.at[0, rows(u), :], loc_sem.at[9]),
        pltpu.make_async_copy(v_hbm.at[:, cols(u * D, D)], kvb.at[1, rows(u), :], loc_sem.at[10]),
    ]
    for copy in loads + own:
        copy.start()

    def clear(i):
        spot = pl.ds(pl.multiple_of(i * T, T), T)
        dqa[0, spot, :] = jnp.zeros((T, D), f32)
        dqa[1, spot, :] = jnp.zeros((T, D), f32)
        dka[:, spot] = jnp.zeros((D, T), f32)
        dva[:, spot] = jnp.zeros((D, T), f32)
        kaug[:, spot] = jnp.zeros((D, T), bf)

    each(0, 2 * U, clear)
    r8 = lax.broadcasted_iota(jnp.int32, (8, T), 0)
    ones_v = jnp.where(jnp.logical_and(r8 >= 4, r8 < 7), 1.0, 0.0)
    for i in range(H // T):
        vaug[:, i * T:(i + 1) * T] = jnp.concatenate(
            [ones_v, jnp.zeros((D - 8, T), f32)], axis=0
        ).astype(bf)

    for copy in loads[:4]:
        copy.wait()
    pl.semaphore_wait(barrier, U - 1 + has_up.astype(jnp.int32) + has_dn.astype(jnp.int32))

    def frm_of(k):
        return lax.rem(u + U - k, U)

    def qd_in(which, h, k, place, peer, dev):
        ref, buf = ((q_in, qb), (do_in, dob))[which]
        return rcopy(
            ref.at[:, cols(peer * GD + h * D, D)], buf.at[rows(place), h * D:(h + 1) * D],
            qd_s.at[which, h, k], qd_r.at[which, h, k], dev,
        )

    def kv_in(which, k, place, peer, dev):
        ref = (k_in, v_in)[which]
        return rcopy(
            ref.at[:, cols(peer * D, D)], kvb.at[which, rows(place), :],
            kv_s.at[which, k], kv_r.at[which, k], dev,
        )

    def st_in(k, place, peer, dev):
        return rcopy(stat_ref.at[peer], statb.at[0, place], st_s.at[k], st_r.at[k], dev)

    def send_qd(h):
        def one(k):
            to = lax.rem(u + k, U)
            for which in range(2):
                qd_in(which, h, k, u, to, at(b, to)).start()
        each(1, U, one)

    def send_kv(k):
        to = lax.rem(u + k, U)
        for which in range(2):
            kv_in(which, k, u, to, at(b, to)).start()

    send_qd(0)
    each(1, U, send_kv)
    send_qd(1)

    for copy in loads[4:]:
        copy.wait()
    lane = lax.broadcasted_iota(jnp.int32, (T, 128), 1)
    table = jnp.zeros((T, 128), f32)
    for h in range(QUERY_HEADS):
        piece = slice(h * D, (h + 1) * D)
        total = jnp.sum(
            do_in[:, piece].astype(f32) * out_in[:, piece].astype(f32), axis=1, keepdims=True
        )
        table = jnp.where(lane == h, total, table)
    table = table.T
    part0, part1 = lp_in[:, 0, :], lp_in[:, 1, :]
    highest = jnp.maximum(part0, part1)
    lse_rows = highest + jnp.log(jnp.exp(part0 - highest) + jnp.exp(part1 - highest))
    id_rows = jnp.broadcast_to(ids_in[...].astype(f32), (8 - 2 * GROUP, T))
    for p in range(U):
        pick = slice(p * GROUP, (p + 1) * GROUP)
        stat_ref[p] = jnp.concatenate([lse_rows[pick], table[pick], id_rows], axis=0)
    statb[0, u] = stat_ref[u]

    def send_st(k):
        to = lax.rem(u + k, U)
        st_in(k, u, to, at(b, to)).start()

    each(1, U, send_st)

    def zq(which, h, place):
        buf = (qb, dob)[which]
        return rcopy(
            buf.at[rows(place), h * D:(h + 1) * D], buf.at[rows(place, R), h * D:(h + 1) * D],
            zq_s.at[which, h, place], zq_r.at[which, h, place], at(b - 1, u),
        )

    def zk(which, place):
        return rcopy(
            kvb.at[which, rows(place), :], kvb.at[which, rows(place, R), :],
            zk_s.at[which, place], zk_r.at[which, place], at(b + 1, u),
        )

    def zst(which):
        dev = (at(b - 1, u), at(b + 1, u))[which]
        return rcopy(statb.at[0], statb.at[1 + which], zst_s.at[which], zst_r.at[which], dev)

    lower = b >= 2

    def relay_q(h, place):
        @pl.when(lower)
        def _():
            for which in range(2):
                zq(which, h, place).start()

    def relay_k(place):
        @pl.when(has_up)
        def _():
            for which in range(2):
                zk(which, place).start()

    def turn_q(h, base):
        def one(p):
            spot = rows(p, base)
            qT[h, :, spot] = qb[spot, h * D:(h + 1) * D].T
            dT[h, :, spot] = dob[spot, h * D:(h + 1) * D].T
        each(0, U, one)

    def turn_k(base):
        def one(p):
            spot = rows(p, base)
            kT[:, spot] = kvb[0, spot, :].T
            vT[:, spot] = kvb[1, spot, :].T
        each(0, U, one)

    def codes(st):
        doc = jnp.broadcast_to(st[4:5, :], (16, T))
        high = jnp.floor(doc * 0.125)
        low = (doc - 8.0 * high)[:8]
        i16 = lax.broadcasted_iota(jnp.int32, (16, T), 0).astype(f32)
        return jnp.where(i16[:8] == low, 1.0, 0.0), jnp.where(i16 == high, 1.0, 0.0)

    def split3(x):
        a = x.astype(bf).astype(f32)
        c = (x - a).astype(bf).astype(f32)
        return a, c, (x - a - c)

    def build_q(which):
        def one(p):
            st = statb[which, p]
            oc, oa = codes(st)
            for h in range(GROUP):
                rows8 = jnp.ones((8, T), f32)
                parts = split3(st[h:h + 1, :] * (-math.sqrt(D)))
                more = split3(-st[GROUP + h:GROUP + h + 1, :])
                for i in range(3):
                    rows8 = jnp.where(r8 == i, parts[i], rows8)
                    rows8 = jnp.where(r8 == 4 + i, more[i], rows8)
                full = jnp.concatenate([rows8, oc, oa, jnp.zeros((D - 32, T), f32)], axis=0)
                aug[h, rows(p, which * R), :] = full.T.astype(bf)
        each(0, U, one)

    def build_k(src, base):
        def one(p):
            oc, oa = codes(statb[src, p])
            rows8 = jnp.where(r8 < 3, 1.0, jnp.where(r8 == 3, -2.0 * FAR, 0.0))
            kaug[0:32, rows(p, base)] = jnp.concatenate(
                [rows8, oc * FAR, oa * FAR], axis=0
            ).astype(bf)
        each(0, U, one)

    own[0].wait()
    own[1].wait()
    relay_q(0, u)

    def got_q(h):
        def one(k):
            frm = frm_of(k)
            for which in range(2):
                qd_in(which, h, k, frm, frm, at(b, frm)).wait_recv()
            relay_q(h, frm)
        each(1, U, one)

    got_q(0)
    own[2].wait()
    own[3].wait()
    relay_k(u)
    relay_q(1, u)
    turn_q(0, 0)

    def got_k(k):
        frm = frm_of(k)
        for which in range(2):
            kv_in(which, k, frm, frm, at(b, frm)).wait_recv()
        relay_k(frm)

    each(1, U, got_k)
    turn_k(0)
    got_q(1)

    def got_st(k):
        frm = frm_of(k)
        st_in(k, frm, frm, at(b, frm)).wait_recv()

    each(1, U, got_st)

    @pl.when(lower)
    def _():
        zst(0).start()

    @pl.when(has_up)
    def _():
        zst(1).start()

    turn_q(1, 0)
    build_q(0)
    build_k(0, 0)

    factor = scale * math.log2(math.e)

    def tile(qi, ki, causal):
        qrow = pl.ds(pl.multiple_of(qi * H, H), H)
        krow = pl.ds(pl.multiple_of(ki * H, H), H)
        ks = jnp.concatenate([kT[:, krow], kaug[:, krow]], axis=0)
        vs = jnp.concatenate([vT[:, krow], vaug[...]], axis=0)
        kn = kvb[0, krow, :]
        dk = dv = None
        for h in range(GROUP):
            extra = aug[h, qrow, :]
            qs = jnp.concatenate([qb[qrow, h * D:(h + 1) * D], extra], axis=1)
            ds = jnp.concatenate([dob[qrow, h * D:(h + 1) * D], extra], axis=1)
            w = jnp.exp2(dot(qs, ks) * factor)
            if causal:
                qpos = lax.broadcasted_iota(jnp.int32, (H, H), 0) + qi * H
                kpos = lax.broadcasted_iota(jnp.int32, (H, H), 1) + ki * H
                w = jnp.where(kpos <= qpos, w, 0.0)
            g = (w * dot(ds, vs)).astype(bf)
            w = w.astype(bf)
            part_v = dot(dT[h, :, qrow], w)
            part_k = dot(qT[h, :, qrow], g)
            dqa[h, qrow, :] += dot(g, kn)
            dv = part_v if dv is None else dv + part_v
            dk = part_k if dk is None else dk + part_k
        dva[:, krow] += dv
        dka[:, krow] += dk

    def near(t):
        tile((t + 1) // 2, t // 2, True)

    each(0, 3, near)

    def give_k(half):
        return rcopy(retk.at[half], ink.at[half], rk_s.at[half], rk_r.at[half], at(b - 1, u))

    def give_q(half):
        return rcopy(retq.at[half], inq.at[half], rq_s.at[half], rq_r.at[half], at(b + 1, u))

    def half_of(half, base=0):
        return slice(base + half * H, base + (half + 1) * H)

    @pl.when(has_dn)
    def _():
        zst(1).wait_recv()

        def one(p):
            for which in range(2):
                zk(which, p).wait_recv()
        each(0, U, one)
        turn_k(R)
        build_k(2, R)
        each(0, 2, lambda t: tile(t, 3, False))

    @pl.when(mid)
    def _():
        zst(0).wait_recv()

        def one(p):
            for h in range(GROUP):
                for which in range(2):
                    zq(which, h, p).wait_recv()
        each(0, U, one)
        for h in range(GROUP):
            turn_q(h, R)
        build_q(1)
        each(0, 2, lambda t: tile(3 - t, 3, False))
        retq[1] = dqa[:, half_of(1, R), :].astype(bf)
        give_q(1).start()

    @pl.when(has_dn)
    def _():
        retk[1, 0] = dka[:, half_of(1, R)].astype(bf)
        retk[1, 1] = dva[:, half_of(1, R)].astype(bf)
        give_k(1).start()
        each(0, jnp.where(has_up, 3, 2), lambda t: tile(t, 2, False))
        retk[0, 0] = dka[:, half_of(0, R)].astype(bf)
        retk[0, 1] = dva[:, half_of(0, R)].astype(bf)
        give_k(0).start()

    @pl.when(mid)
    def _():
        retq[0] = dqa[:, half_of(0, R), :].astype(bf)
        give_q(0).start()

    def oq(place, peer, dev):
        return rcopy(
            dqs.at[rows(place), :], dq_ref.at[:, cols(peer * GD, GD)],
            oq_s.at[place], oq_r.at[peer], dev,
        )

    def okv(which, place, peer, dev):
        ref = (dk_ref, dv_ref)[which]
        return rcopy(
            dkvs.at[which, rows(place), :], ref.at[:, cols(peer * D, D)],
            okv_s.at[which, place], okv_r.at[which, peer], dev,
        )

    def keep_q():
        return pltpu.make_async_copy(
            dqs.at[rows(u), :], dq_ref.at[:, cols(u * GD, GD)], keep_sem.at[2]
        )

    def keep_kv(which):
        ref = (dk_ref, dv_ref)[which]
        return pltpu.make_async_copy(
            dkvs.at[which, rows(u), :], ref.at[:, cols(u * D, D)], keep_sem.at[which]
        )

    Q = U // 2

    def spread(half, start_remote, start_own):
        mine = (u // Q) == half
        for k in range(Q):
            to = half * Q + lax.rem(lax.rem(u, Q) + k, Q)
            if k == 0:
                @pl.when(mine)
                def _():
                    start_own()

                @pl.when(jnp.logical_not(mine))
                def _():
                    start_remote(to)
            else:
                start_remote(to)

    def finish_q(half):
        @pl.when(lower)
        def _():
            give_q(half).wait_recv()
            for h in range(GROUP):
                dqa[h, half_of(half), :] += inq[half, h].astype(f32)
        for h in range(GROUP):
            dqs[half_of(half), h * D:(h + 1) * D] = (dqa[h, half_of(half), :] * scale).astype(bf)
        spread(half, lambda to: oq(to, u, at(b, to)).start(), lambda: keep_q().start())

    def finish_kv(half):
        @pl.when(has_up)
        def _():
            give_k(half).wait_recv()
            dka[:, half_of(half)] += ink[half, 0].astype(f32)
            dva[:, half_of(half)] += ink[half, 1].astype(f32)
        dkvs[0, half_of(half), :] = (dka[:, half_of(half)] * scale).T.astype(bf)
        dkvs[1, half_of(half), :] = dva[:, half_of(half)].T.astype(bf)

        def go(to):
            for which in range(2):
                okv(which, to, u, at(b, to)).start()

        def stay():
            for which in range(2):
                keep_kv(which).start()

        spread(half, go, stay)

    for half in (1, 0):
        finish_q(half)
        finish_kv(half)

    keep_q().wait()
    for which in range(2):
        keep_kv(which).wait()

    def drain(k):
        to, frm = lax.rem(u + k, U), frm_of(k)
        for which in range(2):
            for h in range(GROUP):
                qd_in(which, h, k, u, to, at(b, to)).wait_send()
            kv_in(which, k, u, to, at(b, to)).wait_send()
        st_in(k, u, to, at(b, to)).wait_send()
        oq(to, u, at(b, to)).wait_send()
        oq(u, frm, at(b, frm)).wait_recv()
        for which in range(2):
            okv(which, to, u, at(b, to)).wait_send()
            okv(which, u, frm, at(b, frm)).wait_recv()

    each(1, U, drain)

    @pl.when(lower)
    def _():
        zst(0).wait_send()

        def one(p):
            for which in range(2):
                for h in range(GROUP):
                    zq(which, h, p).wait_send()
        each(0, U, one)

    @pl.when(has_up)
    def _():
        zst(1).wait_send()

        def one(p):
            for which in range(2):
                zk(which, p).wait_send()
        each(0, U, one)

    @pl.when(has_dn)
    def _():
        for half in range(2):
            give_k(half).wait_send()

    @pl.when(mid)
    def _():
        for half in range(2):
            give_q(half).wait_send()


def close_kernel(a_in, b_in, c_in, a_out, b_out, c_out, a_mid, b_mid, c_mid, in_sem, out_sem):
    moves = []
    for i, (src, mid, dst) in enumerate(
        [(a_in, a_mid, a_out), (b_in, b_mid, b_out), (c_in, c_mid, c_out)]
    ):
        height = src.shape[0] // PIECES
        for n in range(PIECES):
            part = pl.ds(n * height, height)
            moves.append((
                pltpu.make_async_copy(src.at[part], mid.at[part], in_sem.at[i, n]),
                pltpu.make_async_copy(mid.at[part], dst.at[part], out_sem.at[i, n]),
            ))
    for load, _ in moves:
        load.start()
    for load, store in moves:
        load.wait()
        store.start()
    for _, store in moves:
        store.wait()


def per_device(uly_count, blk_count, q, k, v, out, grad, lse_parts, segment_ids):
    U, B = uly_count, blk_count
    T = q.shape[0]
    R = T * U
    D = HEAD_SIZE
    GD = GROUP * D
    assert KEY_VALUE_HEADS == U
    parts = lse_parts.transpose(1, 2, 0)
    ids = segment_ids.reshape(1, T)
    bf, f32 = jnp.bfloat16, jnp.float32
    dma = pltpu.SemaphoreType.DMA
    sems = []
    for shape in [(2, 2, U), (2, U), (U,), (2, 2, U), (2, U), (2,), (2,), (2,), (U,), (2, U)]:
        sems += [dma(shape), dma(shape)]
    vm = pltpu.VMEM
    results = pl.pallas_call(
        functools.partial(kernel, U, B),
        out_shape=(
            jax.ShapeDtypeStruct(q.shape, bf),
            jax.ShapeDtypeStruct(k.shape, bf),
            jax.ShapeDtypeStruct(v.shape, bf),
        ),
        in_specs=[pl.BlockSpec(memory_space=pltpu.HBM)] * 7,
        out_specs=tuple([pl.BlockSpec(memory_space=pltpu.HBM)] * 3),
        scratch_shapes=[
            vm(q.shape, bf), vm(q.shape, bf), vm(k.shape, bf), vm(v.shape, bf),
            vm(q.shape, bf), vm(parts.shape, f32), vm((1, T), jnp.int32),
            vm((2 * R, GD), bf), vm((2 * R, GD), bf), vm((2, 2 * R, D), bf),
            vm((U, 8, T), f32), vm((3, U, 8, T), f32),
            vm((GROUP, 2 * R, D), bf), vm((D, 2 * R), bf), vm((D, R // 2), bf),
            vm((GROUP, D, 2 * R), bf), vm((GROUP, D, 2 * R), bf),
            vm((D, 2 * R), bf), vm((D, 2 * R), bf),
            vm((GROUP, 2 * R, D), f32), vm((D, 2 * R), f32), vm((D, 2 * R), f32),
            vm((2, 2, D, R // 2), bf), vm((2, GROUP, R // 2, D), bf),
            vm((2, 2, D, R // 2), bf), vm((2, GROUP, R // 2, D), bf),
            vm((R, GD), bf), vm((2, R, D), bf),
            dma((11,)), dma((3,)),
        ] + sems,
        compiler_params=pltpu.CompilerParams(
            collective_id=0, has_side_effects=True, vmem_limit_bytes=60 << 20
        ),
    )(q, grad, k, v, out, parts, ids)
    hbm = [pl.BlockSpec(memory_space=pltpu.HBM)] * 3
    return pl.pallas_call(
        close_kernel,
        out_shape=tuple(jax.ShapeDtypeStruct(r.shape, r.dtype) for r in results),
        in_specs=hbm,
        out_specs=tuple(hbm),
        scratch_shapes=[vm(r.shape, r.dtype) for r in results]
        + [dma((3, PIECES)), dma((3, PIECES))],
        compiler_params=pltpu.CompilerParams(vmem_limit_bytes=56 << 20),
    )(*results)


def solution(mesh):
    spec = P(("blk", "uly"), None)
    body = functools.partial(per_device, mesh.shape["uly"], mesh.shape["blk"])
    return jax.shard_map(
        body,
        mesh=mesh,
        in_specs=(spec, spec, spec, spec, spec, P(("blk", "uly"), None, None), P(("blk", "uly"))),
        out_specs=(spec, spec, spec),
        check_vma=False,
    )
```

time: 119 us -> 78.9 us (0.66)
  Pallas kernels: 118 us -> 78.1 us
    pallas_call x1, Pallas kernels: 116 us -> 76.1 us  [per_device(): pl.pallas_call(functools.partial(kernel, U, B), out_shape=(jax.ShapeDtype...]
where the time goes in v1:
time: 78.9 us; the launch traced here: 78.8 us
  Pallas kernels  78.1 us (99%)
    pallas_call x1, Pallas kernels, per_device(): pl.pallas_call(functools.partial(kernel, U, B), out_shape=(jax.ShapeDtype...  76.1 us
    pallas_call x1, Pallas kernels, per_device(): pl.pallas_call(close_kernel, out_shape=tuple((jax.ShapeDtypeStruct(r.shap...  2.01 us

profile of v1, /device:TPU:7, one launch (start us, length us, event | category | flops | bytes accessed | tf_op | source)
XLA Modules:
  0.0 78.8 jit_solution(9910326172804658000)
XLA Ops:
  0.6 76.1 %shard_map.94 = (bf16[128,2048]{1,0:T(8,128)(2,1)}, bf16[128,1024]{1,0:T(8,128)(2,1)}, bf16[128,1024]{1,0:T(8,128)(2,1)}) custom-call(bf16[128,2048]{1,0:T(8,128)(2,1)} %q_hbm.1, bf16[128,2048]{1,0:T(8,128)(2,1)} %do_hbm.1, bf16[128,1024]{1,0:T(8,128)(2,1)} %k_hbm.1, bf16[128,1024]{1,0:T(8,128)(2,1)} %v_hbm.1, bf16[128,2048]{1,0:T(8,128)(2,1)} %out_hbm.1, ...), custom_call_target="tpu_custom_call" | custom-call | tf_op jit(solution)/shard_map/pallas_call | solution.py:556
  76.7 2.0 %shard_map.95 = (bf16[128,2048]{1,0:T(8,128)(2,1)}, bf16[128,1024]{1,0:T(8,128)(2,1)}, bf16[128,1024]{1,0:T(8,128)(2,1)}) custom-call(bf16[128,2048]{1,0:T(8,128)(2,1)} %get-tuple-element.6.a_in, bf16[128,1024]{1,0:T(8,128)(2,1)} %get-tuple-element.7.b_in, bf16[128,1024]{1,0:T(8,128)(2,1)} %get-tuple-element.8.c_in), custom_call_target="tpu_custom_call" | custom-call | tf_op jit(solution)/shard_map/pallas_call | solution.py:584

commit v2 on v1

--- a/solution.py
+++ b/solution.py
@@ -14,6 +14,7 @@
 GROUP = QUERY_HEADS // KEY_VALUE_HEADS
 PIECES = 2
 FAR = 8192.0
+LAYER = 16
 
 
 def dot(a, b):
@@ -29,7 +30,7 @@
     aug, kaug, vaug, qT, dT, kT, vT,
     dqa, dka, dva,
     retk, retq, ink, inq, dqs, dkvs,
-    loc_sem, keep_sem,
+    loc_sem, keep_sem, ready,
     qd_s, qd_r, kv_s, kv_r, st_s, st_r,
     zq_s, zq_r, zk_s, zk_r, zst_s, zst_r,
     rk_s, rk_r, rq_s, rq_r, oq_s, oq_r, okv_s, okv_r,
@@ -75,10 +76,6 @@
             barrier, inc=1, device_id=at(b, lax.rem(u + k, U)), device_id_type=pl.DeviceIdType.MESH
         )
 
-    @pl.when(has_up)
-    def _():
-        pl.semaphore_signal(barrier, inc=1, device_id=at(b + 1, u), device_id_type=pl.DeviceIdType.MESH)
-
     @pl.when(has_dn)
     def _():
         pl.semaphore_signal(barrier, inc=1, device_id=at(b - 1, u), device_id_type=pl.DeviceIdType.MESH)
@@ -117,7 +114,11 @@
 
     for copy in loads[:4]:
         copy.wait()
-    pl.semaphore_wait(barrier, U - 1 + has_up.astype(jnp.int32) + has_dn.astype(jnp.int32))
+    pl.semaphore_wait(barrier, U - 1 + has_up.astype(jnp.int32))
+
+    @pl.when(has_up)
+    def _():
+        pl.semaphore_signal(ready, inc=1, device_id=at(b + 1, u), device_id_type=pl.DeviceIdType.MESH)
 
     def frm_of(k):
         return lax.rem(u + U - k, U)
@@ -126,18 +127,26 @@
         ref, buf = ((q_in, qb), (do_in, dob))[which]
         return rcopy(
             ref.at[:, cols(peer * GD + h * D, D)], buf.at[rows(place), h * D:(h + 1) * D],
-            qd_s.at[which, h, k], qd_r.at[which, h, k], dev,
+            qd_s.at[0], qd_r.at[h, k], dev,
         )
 
     def kv_in(which, k, place, peer, dev):
         ref = (k_in, v_in)[which]
         return rcopy(
             ref.at[:, cols(peer * D, D)], kvb.at[which, rows(place), :],
-            kv_s.at[which, k], kv_r.at[which, k], dev,
+            kv_s.at[0], kv_r.at[k], dev,
         )
 
     def st_in(k, place, peer, dev):
-        return rcopy(stat_ref.at[peer], statb.at[0, place], st_s.at[k], st_r.at[k], dev)
+        return rcopy(stat_ref.at[peer], statb.at[0, place], st_s.at[0], st_r.at[0], dev)
+
+    def many(height, width, sem):
+        part = qb.at[pl.ds(0, height * width // GD), :]
+        pltpu.make_async_copy(part, part, sem).wait()
+
+    def stat_wait(sem):
+        part = statb.at[0, pl.ds(0, U - 1)]
+        pltpu.make_async_copy(part, part, sem).wait()
 
     def send_qd(h):
         def one(k):
@@ -153,7 +162,6 @@
 
     send_qd(0)
     each(1, U, send_kv)
-    send_qd(1)
 
     for copy in loads[4:]:
         copy.wait()
@@ -180,18 +188,19 @@
         st_in(k, u, to, at(b, to)).start()
 
     each(1, U, send_st)
+    send_qd(1)
 
     def zq(which, h, place):
         buf = (qb, dob)[which]
         return rcopy(
             buf.at[rows(place), h * D:(h + 1) * D], buf.at[rows(place, R), h * D:(h + 1) * D],
-            zq_s.at[which, h, place], zq_r.at[which, h, place], at(b - 1, u),
+            zq_s.at[0], zq_r.at[h], at(b - 1, u),
         )
 
     def zk(which, place):
         return rcopy(
             kvb.at[which, rows(place), :], kvb.at[which, rows(place, R), :],
-            zk_s.at[which, place], zk_r.at[which, place], at(b + 1, u),
+            zk_s.at[0], zk_r.at[0], at(b + 1, u),
         )
 
     def zst(which):
@@ -199,9 +208,11 @@
         return rcopy(statb.at[0], statb.at[1 + which], zst_s.at[which], zst_r.at[which], dev)
 
     lower = b >= 2
+    late = lax.rem(b, LAYER) == 0
+    late_q = jnp.logical_and(lower, late)
 
     def relay_q(h, place):
-        @pl.when(lower)
+        @pl.when(jnp.logical_and(lower, jnp.logical_not(late)) if h == 0 else lower)
         def _():
             for which in range(2):
                 zq(which, h, place).start()
@@ -264,13 +275,17 @@
 
     own[0].wait()
     own[1].wait()
+
+    @pl.when(jnp.logical_and(has_dn, jnp.logical_not(late)))
+    def _():
+        pl.semaphore_wait(ready, 1)
+
     relay_q(0, u)
 
     def got_q(h):
         def one(k):
             frm = frm_of(k)
-            for which in range(2):
-                qd_in(which, h, k, frm, frm, at(b, frm)).wait_recv()
+            many(2 * T, D, qd_r.at[h, k])
             relay_q(h, frm)
         each(1, U, one)
 
@@ -278,24 +293,28 @@
     own[2].wait()
     own[3].wait()
     relay_k(u)
+    turn_q(0, 0)
+
+    @pl.when(jnp.logical_and(has_dn, late))
+    def _():
+        pl.semaphore_wait(ready, 1)
+
+    @pl.when(late_q)
+    def _():
+        def one(p):
+            for which in range(2):
+                zq(which, 0, p).start()
+        each(0, U, one)
+
     relay_q(1, u)
-    turn_q(0, 0)
 
     def got_k(k):
-        frm = frm_of(k)
-        for which in range(2):
-            kv_in(which, k, frm, frm, at(b, frm)).wait_recv()
-        relay_k(frm)
+        many(2 * T, D, kv_r.at[k])
+        relay_k(frm_of(k))
 
     each(1, U, got_k)
     turn_k(0)
-    got_q(1)
-
-    def got_st(k):
-        frm = frm_of(k)
-        st_in(k, frm, frm, at(b, frm)).wait_recv()
-
-    each(1, U, got_st)
+    stat_wait(st_r.at[0])
 
     @pl.when(lower)
     def _():
@@ -305,20 +324,19 @@
     def _():
         zst(1).start()
 
-    turn_q(1, 0)
     build_q(0)
     build_k(0, 0)
 
     factor = scale * math.log2(math.e)
 
-    def tile(qi, ki, causal):
+    def tile(qi, ki, causal, heads=(0, 1)):
         qrow = pl.ds(pl.multiple_of(qi * H, H), H)
         krow = pl.ds(pl.multiple_of(ki * H, H), H)
         ks = jnp.concatenate([kT[:, krow], kaug[:, krow]], axis=0)
         vs = jnp.concatenate([vT[:, krow], vaug[...]], axis=0)
         kn = kvb[0, krow, :]
         dk = dv = None
-        for h in range(GROUP):
+        for h in heads:
             extra = aug[h, qrow, :]
             qs = jnp.concatenate([qb[qrow, h * D:(h + 1) * D], extra], axis=1)
             ds = jnp.concatenate([dob[qrow, h * D:(h + 1) * D], extra], axis=1)
@@ -337,79 +355,93 @@
         dva[:, krow] += dv
         dka[:, krow] += dk
 
-    def near(t):
-        tile((t + 1) // 2, t // 2, True)
-
-    each(0, 3, near)
-
-    def give_k(half):
-        return rcopy(retk.at[half], ink.at[half], rk_s.at[half], rk_r.at[half], at(b - 1, u))
-
-    def give_q(half):
-        return rcopy(retq.at[half], inq.at[half], rq_s.at[half], rq_r.at[half], at(b + 1, u))
+    each(0, 3, lambda t: tile((t + 1) // 2, t // 2, True, (0,)))
+    got_q(1)
+    turn_q(1, 0)
+    each(0, 3, lambda t: tile((t + 1) // 2, t // 2, True, (1,)))
+
+    def give_k(half, which):
+        return rcopy(
+            retk.at[half, which], ink.at[half, which],
+            rk_s.at[half, which], rk_r.at[half, which], at(b - 1, u),
+        )
+
+    def give_q(half, h):
+        return rcopy(
+            retq.at[half, h], inq.at[half, h],
+            rq_s.at[half, h], rq_r.at[half, h], at(b + 1, u),
+        )
 
     def half_of(half, base=0):
         return slice(base + half * H, base + (half + 1) * H)
 
+    def return_k(which, half):
+        total = (dka, dva)[which]
+        retk[half, which] = total[:, half_of(half, R)].astype(bf)
+        give_k(half, which).start()
+
+    def return_q(half, h):
+        retq[half, h] = dqa[h, half_of(half, R), :].astype(bf)
+        give_q(half, h).start()
+
     @pl.when(has_dn)
     def _():
         zst(1).wait_recv()
-
-        def one(p):
-            for which in range(2):
-                zk(which, p).wait_recv()
-        each(0, U, one)
+        many(2 * R, D, zk_r.at[0])
         turn_k(R)
         build_k(2, R)
-        each(0, 2, lambda t: tile(t, 3, False))
+        each(0, 4, lambda t: tile(t % 2, 3 - t // 2, False))
 
     @pl.when(mid)
     def _():
         zst(0).wait_recv()
-
-        def one(p):
-            for h in range(GROUP):
-                for which in range(2):
-                    zq(which, h, p).wait_recv()
-        each(0, U, one)
+        build_q(1)
         for h in range(GROUP):
+            many(2 * R, D, zq_r.at[h])
             turn_q(h, R)
-        build_q(1)
-        each(0, 2, lambda t: tile(3 - t, 3, False))
-        retq[1] = dqa[:, half_of(1, R), :].astype(bf)
-        give_q(1).start()
-
-    @pl.when(has_dn)
-    def _():
-        retk[1, 0] = dka[:, half_of(1, R)].astype(bf)
-        retk[1, 1] = dva[:, half_of(1, R)].astype(bf)
-        give_k(1).start()
-        each(0, jnp.where(has_up, 3, 2), lambda t: tile(t, 2, False))
-        retk[0, 0] = dka[:, half_of(0, R)].astype(bf)
-        retk[0, 1] = dva[:, half_of(0, R)].astype(bf)
-        give_k(0).start()
-
-    @pl.when(mid)
-    def _():
-        retq[0] = dqa[:, half_of(0, R), :].astype(bf)
-        give_q(0).start()
-
-    def oq(place, peer, dev):
-        return rcopy(
-            dqs.at[rows(place), :], dq_ref.at[:, cols(peer * GD, GD)],
-            oq_s.at[place], oq_r.at[peer], dev,
+
+        def far(t):
+            tile(3 - (t + 1) // 2, 3 - t // 2, False)
+
+            @pl.when(t == 0)
+            def _():
+                for h in range(GROUP):
+                    return_q(1, h)
+
+            @pl.when(t == 1)
+            def _():
+                return_k(1, 1)
+
+        each(0, 3, far)
+        return_q(0, 0)
+        return_k(1, 0)
+        return_q(0, 1)
+        return_k(0, 1)
+        return_k(0, 0)
+
+    @pl.when(jnp.logical_and(has_dn, jnp.logical_not(has_up)))
+    def _():
+        for which in (1, 0):
+            for half in (1, 0):
+                return_k(which, half)
+
+    def oq(h, place, peer, dev):
+        return rcopy(
+            dqs.at[rows(place), h * D:(h + 1) * D], dq_ref.at[:, cols(peer * GD + h * D, D)],
+            oq_s.at[0], oq_r.at[0], dev,
         )
 
     def okv(which, place, peer, dev):
         ref = (dk_ref, dv_ref)[which]
         return rcopy(
             dkvs.at[which, rows(place), :], ref.at[:, cols(peer * D, D)],
-            okv_s.at[which, place], okv_r.at[which, peer], dev,
-        )
-
-    def keep_q():
+            okv_s.at[0], okv_r.at[which], dev,
+        )
+
+    def keep_q(h):
         return pltpu.make_async_copy(
-            dqs.at[rows(u), :], dq_ref.at[:, cols(u * GD, GD)], keep_sem.at[2]
+            dqs.at[rows(u), h * D:(h + 1) * D], dq_ref.at[:, cols(u * GD + h * D, D)],
+            keep_sem.at[2 + h],
         )
 
     def keep_kv(which):
@@ -418,103 +450,82 @@
             dkvs.at[which, rows(u), :], ref.at[:, cols(u * D, D)], keep_sem.at[which]
         )
 
-    Q = U // 2
-
-    def spread(half, start_remote, start_own):
-        mine = (u // Q) == half
-        for k in range(Q):
-            to = half * Q + lax.rem(lax.rem(u, Q) + k, Q)
-            if k == 0:
-                @pl.when(mine)
-                def _():
-                    start_own()
-
-                @pl.when(jnp.logical_not(mine))
-                def _():
-                    start_remote(to)
-            else:
-                start_remote(to)
-
-    def finish_q(half):
+    def finish_q(h):
         @pl.when(lower)
         def _():
-            give_q(half).wait_recv()
-            for h in range(GROUP):
+            for half in (1, 0):
+                give_q(half, h).wait_recv()
                 dqa[h, half_of(half), :] += inq[half, h].astype(f32)
-        for h in range(GROUP):
-            dqs[half_of(half), h * D:(h + 1) * D] = (dqa[h, half_of(half), :] * scale).astype(bf)
-        spread(half, lambda to: oq(to, u, at(b, to)).start(), lambda: keep_q().start())
-
-    def finish_kv(half):
+        dqs[:, h * D:(h + 1) * D] = (dqa[h, 0:R, :] * scale).astype(bf)
+
+        def go(k):
+            to = lax.rem(u + k, U)
+            oq(h, to, u, at(b, to)).start()
+
+        each(1, U, go)
+        keep_q(h).start()
+
+    def finish_kv(which):
+        total = (dka, dva)[which]
+
         @pl.when(has_up)
         def _():
-            give_k(half).wait_recv()
-            dka[:, half_of(half)] += ink[half, 0].astype(f32)
-            dva[:, half_of(half)] += ink[half, 1].astype(f32)
-        dkvs[0, half_of(half), :] = (dka[:, half_of(half)] * scale).T.astype(bf)
-        dkvs[1, half_of(half), :] = dva[:, half_of(half)].T.astype(bf)
-
-        def go(to):
-            for which in range(2):
-                okv(which, to, u, at(b, to)).start()
-
-        def stay():
-            for which in range(2):
-                keep_kv(which).start()
-
-        spread(half, go, stay)
-
-    for half in (1, 0):
-        finish_q(half)
-        finish_kv(half)
-
-    keep_q().wait()
+            for half in (1, 0):
+                give_k(half, which).wait_recv()
+                total[:, half_of(half)] += ink[half, which].astype(f32)
+        for half in (1, 0):
+            value = total[:, half_of(half)]
+            if which == 0:
+                value = value * scale
+            dkvs[which, half_of(half), :] = value.T.astype(bf)
+
+        def go(k):
+            to = lax.rem(u + k, U)
+            okv(which, to, u, at(b, to)).start()
+
+        each(1, U, go)
+        keep_kv(which).start()
+
+    finish_q(0)
+    finish_kv(1)
+    finish_q(1)
+    finish_kv(0)
+    for h in range(GROUP):
+        keep_q(h).wait()
     for which in range(2):
         keep_kv(which).wait()
 
-    def drain(k):
-        to, frm = lax.rem(u + k, U), frm_of(k)
-        for which in range(2):
+    many((U - 1) * 4 * T, D, qd_s.at[0])
+    many((U - 1) * 2 * T, D, kv_s.at[0])
+    stat_wait(st_s.at[0])
+
+    @pl.when(lower)
+    def _():
+        zst(0).wait_send()
+        many(4 * R, D, zq_s.at[0])
+
+    @pl.when(has_up)
+    def _():
+        zst(1).wait_send()
+        many(2 * R, D, zk_s.at[0])
+
+    @pl.when(has_dn)
+    def _():
+        for half in range(2):
+            for which in range(2):
+                give_k(half, which).wait_send()
+
+    @pl.when(mid)
+    def _():
+        for half in range(2):
             for h in range(GROUP):
-                qd_in(which, h, k, u, to, at(b, to)).wait_send()
-            kv_in(which, k, u, to, at(b, to)).wait_send()
-        st_in(k, u, to, at(b, to)).wait_send()
-        oq(to, u, at(b, to)).wait_send()
-        oq(u, frm, at(b, frm)).wait_recv()
-        for which in range(2):
-            okv(which, to, u, at(b, to)).wait_send()
-            okv(which, u, frm, at(b, frm)).wait_recv()
-
-    each(1, U, drain)
-
-    @pl.when(lower)
-    def _():
-        zst(0).wait_send()
-
-        def one(p):
-            for which in range(2):
-                for h in range(GROUP):
-                    zq(which, h, p).wait_send()
-        each(0, U, one)
-
-    @pl.when(has_up)
-    def _():
-        zst(1).wait_send()
-
-        def one(p):
-            for which in range(2):
-                zk(which, p).wait_send()
-        each(0, U, one)
-
-    @pl.when(has_dn)
-    def _():
-        for half in range(2):
-            give_k(half).wait_send()
-
-    @pl.when(mid)
-    def _():
-        for half in range(2):
-            give_q(half).wait_send()
+                give_q(half, h).wait_send()
+
+    many((U - 1) * T, GD, oq_s.at[0])
+    many((U - 1) * 2 * T, D, okv_s.at[0])
+    many((U - 1) * T, GD, oq_r.at[0])
+    for which in range(2):
+        many((U - 1) * T, D, okv_r.at[which])
 
 
 def close_kernel(a_in, b_in, c_in, a_out, b_out, c_out, a_mid, b_mid, c_mid, in_sem, out_sem):
@@ -550,8 +561,11 @@
     bf, f32 = jnp.bfloat16, jnp.float32
     dma = pltpu.SemaphoreType.DMA
     sems = []
-    for shape in [(2, 2, U), (2, U), (U,), (2, 2, U), (2, U), (2,), (2,), (2,), (U,), (2, U)]:
-        sems += [dma(shape), dma(shape)]
+    for sent, got in [
+        ((1,), (GROUP, U)), ((1,), (U,)), ((1,), (1,)), ((1,), (GROUP,)), ((1,), (1,)),
+        ((2,), (2,)), ((2, 2), (2, 2)), ((2, 2), (2, 2)), ((1,), (1,)), ((1,), (2,)),
+    ]:
+        sems += [dma(sent), dma(got)]
     vm = pltpu.VMEM
     results = pl.pallas_call(
         functools.partial(kernel, U, B),
@@ -574,7 +588,7 @@
             vm((2, 2, D, R // 2), bf), vm((2, GROUP, R // 2, D), bf),
             vm((2, 2, D, R // 2), bf), vm((2, GROUP, R // 2, D), bf),
             vm((R, GD), bf), vm((2, R, D), bf),
-            dma((11,)), dma((3,)),
+            dma((11,)), dma((4,)), pltpu.SemaphoreType.REGULAR,
         ] + sems,
         compiler_params=pltpu.CompilerParams(
             collective_id=0, has_side_effects=True, vmem_limit_bytes=60 << 20

time: 78.9 us -> 73.2 us (0.928)
  Pallas kernels: 78.1 us -> 72.3 us
    pallas_call x1, Pallas kernels: 76.1 us -> 70.3 us  [per_device(): pl.pallas_call(functools.partial(kernel, U, B), out_shape=(jax.ShapeDtype...]
where the time goes in v2:
time: 73.2 us; the launch traced here: 73 us
  Pallas kernels  72.3 us (99%)
    pallas_call x1, Pallas kernels, per_device(): pl.pallas_call(functools.partial(kernel, U, B), out_shape=(jax.ShapeDtype...  70.3 us
    pallas_call x1, Pallas kernels, per_device(): pl.pallas_call(close_kernel, out_shape=tuple((jax.ShapeDtypeStruct(r.shap...  2.01 us

profile of v2, /device:TPU:7, one launch (start us, length us, event | category | flops | bytes accessed | tf_op | source)
XLA Modules:
  0.0 73.0 jit_solution(4797704076801586869)
XLA Ops:
  0.6 70.3 %shard_map.94 = (bf16[128,2048]{1,0:T(8,128)(2,1)}, bf16[128,1024]{1,0:T(8,128)(2,1)}, bf16[128,1024]{1,0:T(8,128)(2,1)}) custom-call(bf16[128,2048]{1,0:T(8,128)(2,1)} %q_hbm.1, bf16[128,2048]{1,0:T(8,128)(2,1)} %do_hbm.1, bf16[128,1024]{1,0:T(8,128)(2,1)} %k_hbm.1, bf16[128,1024]{1,0:T(8,128)(2,1)} %v_hbm.1, bf16[128,2048]{1,0:T(8,128)(2,1)} %out_hbm.1, ...), custom_call_target="tpu_custom_call" | custom-call | tf_op jit(solution)/shard_map/pallas_call | solution.py:570
  71.0 2.0 %shard_map.95 = (bf16[128,2048]{1,0:T(8,128)(2,1)}, bf16[128,1024]{1,0:T(8,128)(2,1)}, bf16[128,1024]{1,0:T(8,128)(2,1)}) custom-call(bf16[128,2048]{1,0:T(8,128)(2,1)} %get-tuple-element.6.a_in, bf16[128,1024]{1,0:T(8,128)(2,1)} %get-tuple-element.7.b_in, bf16[128,1024]{1,0:T(8,128)(2,1)} %get-tuple-element.8.c_in), custom_call_target="tpu_custom_call" | custom-call | tf_op jit(solution)/shard_map/pallas_call | solution.py:598

commit v3 on v2

--- a/solution.py
+++ b/solution.py
@@ -15,6 +15,7 @@
 PIECES = 2
 FAR = 8192.0
 LAYER = 16
+UNROLL = 4
 
 
 def dot(a, b):
@@ -64,11 +65,11 @@
     def rows(place, base=0):
         return pl.ds(pl.multiple_of(base + place * T, T), T)
 
-    def each(low, high, step):
+    def each(low, high, step, unroll=1):
         def body(i, c):
             step(i)
             return c
-        lax.fori_loop(low, high, body, 0)
+        lax.fori_loop(low, high, body, 0, unroll=unroll)
 
     barrier = pltpu.get_barrier_semaphore()
     for k in range(1, U):
@@ -161,7 +162,6 @@
             kv_in(which, k, u, to, at(b, to)).start()
 
     send_qd(0)
-    each(1, U, send_kv)
 
     for copy in loads[4:]:
         copy.wait()
@@ -188,6 +188,7 @@
         st_in(k, u, to, at(b, to)).start()
 
     each(1, U, send_st)
+    each(1, U, send_kv)
     send_qd(1)
 
     def zq(which, h, place):
@@ -228,14 +229,14 @@
             spot = rows(p, base)
             qT[h, :, spot] = qb[spot, h * D:(h + 1) * D].T
             dT[h, :, spot] = dob[spot, h * D:(h + 1) * D].T
-        each(0, U, one)
+        each(0, U, one, UNROLL)
 
     def turn_k(base):
         def one(p):
             spot = rows(p, base)
             kT[:, spot] = kvb[0, spot, :].T
             vT[:, spot] = kvb[1, spot, :].T
-        each(0, U, one)
+        each(0, U, one, UNROLL)
 
     def codes(st):
         doc = jnp.broadcast_to(st[4:5, :], (16, T))
@@ -262,7 +263,7 @@
                     rows8 = jnp.where(r8 == 4 + i, more[i], rows8)
                 full = jnp.concatenate([rows8, oc, oa, jnp.zeros((D - 32, T), f32)], axis=0)
                 aug[h, rows(p, which * R), :] = full.T.astype(bf)
-        each(0, U, one)
+        each(0, U, one, UNROLL)
 
     def build_k(src, base):
         def one(p):
@@ -271,7 +272,7 @@
             kaug[0:32, rows(p, base)] = jnp.concatenate(
                 [rows8, oc * FAR, oa * FAR], axis=0
             ).astype(bf)
-        each(0, U, one)
+        each(0, U, one, UNROLL)
 
     own[0].wait()
     own[1].wait()
@@ -336,16 +337,19 @@
         vs = jnp.concatenate([vT[:, krow], vaug[...]], axis=0)
         kn = kvb[0, krow, :]
         dk = dv = None
+        raw = []
         for h in heads:
             extra = aug[h, qrow, :]
             qs = jnp.concatenate([qb[qrow, h * D:(h + 1) * D], extra], axis=1)
             ds = jnp.concatenate([dob[qrow, h * D:(h + 1) * D], extra], axis=1)
-            w = jnp.exp2(dot(qs, ks) * factor)
+            raw.append((dot(qs, ks), dot(ds, vs)))
+        for h, (score, prob) in zip(heads, raw):
+            w = jnp.exp2(score * factor)
             if causal:
                 qpos = lax.broadcasted_iota(jnp.int32, (H, H), 0) + qi * H
                 kpos = lax.broadcasted_iota(jnp.int32, (H, H), 1) + ki * H
                 w = jnp.where(kpos <= qpos, w, 0.0)
-            g = (w * dot(ds, vs)).astype(bf)
+            g = (w * prob).astype(bf)
             w = w.astype(bf)
             part_v = dot(dT[h, :, qrow], w)
             part_k = dot(qT[h, :, qrow], g)
@@ -384,46 +388,66 @@
         retq[half, h] = dqa[h, half_of(half, R), :].astype(bf)
         give_q(half, h).start()
 
-    @pl.when(has_dn)
-    def _():
-        zst(1).wait_recv()
-        many(2 * R, D, zk_r.at[0])
-        turn_k(R)
-        build_k(2, R)
-        each(0, 4, lambda t: tile(t % 2, 3 - t // 2, False))
-
-    @pl.when(mid)
-    def _():
+    def take_next():
         zst(0).wait_recv()
         build_q(1)
         for h in range(GROUP):
             many(2 * R, D, zq_r.at[h])
             turn_q(h, R)
 
-        def far(t):
-            tile(3 - (t + 1) // 2, 3 - t // 2, False)
-
-            @pl.when(t == 0)
+    def pick(t, table):
+        out = table[0]
+        for i, value in enumerate(table[1:]):
+            out = jnp.where(t > i, value, out)
+        return out
+
+    late_i, mid_i = late.astype(jnp.int32), mid.astype(jnp.int32)
+    edge = lax.rem(b, LAYER) == LAYER - 1
+    first_c = jnp.where(edge, 2, 3) * (1 - late_i)
+    last_c = first_c + 2
+    last = 3 + 3 * mid_i
+    last_v = jnp.where(edge, 1 + 2 * mid_i, 4)
+
+    @pl.when(has_dn)
+    def _():
+        zst(1).wait_recv()
+        many(2 * R, D, zk_r.at[0])
+        turn_k(R)
+        build_k(2, R)
+
+        def step(t):
+            @pl.when(jnp.logical_and(mid, t == first_c))
             def _():
-                for h in range(GROUP):
-                    return_q(1, h)
-
-            @pl.when(t == 1)
+                take_next()
+
+            c = t - first_c
+            is_c = jnp.logical_and(mid, jnp.logical_and(c >= 0, c < 3))
+            n = t - jnp.where(jnp.logical_and(mid, c >= 3), 3, 0)
+            qi = jnp.where(is_c, pick(c, (3, 2, 2)), n % 2)
+            ki = jnp.where(is_c, pick(c, (3, 3, 2)), 3 - n // 2)
+            tile(qi, ki, False)
+
+            @pl.when(jnp.logical_and(mid, t == first_c))
+            def _():
+                return_q(1, 0)
+
+            @pl.when(jnp.logical_and(mid, t == last_c))
+            def _():
+                return_q(0, 0)
+                return_q(1, 1)
+                return_q(0, 1)
+
+            @pl.when(t == last_v)
             def _():
                 return_k(1, 1)
 
-        each(0, 3, far)
-        return_q(0, 0)
-        return_k(1, 0)
-        return_q(0, 1)
-        return_k(0, 1)
-        return_k(0, 0)
-
-    @pl.when(jnp.logical_and(has_dn, jnp.logical_not(has_up)))
-    def _():
-        for which in (1, 0):
-            for half in (1, 0):
-                return_k(which, half)
+            @pl.when(t == last)
+            def _():
+                return_k(1, 0)
+                return_k(0, 1)
+                return_k(0, 0)
+
+        each(0, last + 1, step)
 
     def oq(h, place, peer, dev):
         return rcopy(
@@ -486,41 +510,53 @@
         each(1, U, go)
         keep_kv(which).start()
 
-    finish_q(0)
+    @pl.when(jnp.logical_not(late))
+    def _():
+        finish_q(0)
+
     finish_kv(1)
-    finish_q(1)
+
+    @pl.when(jnp.logical_not(late))
+    def _():
+        finish_q(1)
+
     finish_kv(0)
+
+    @pl.when(late)
+    def _():
+        for h in range(GROUP):
+            finish_q(h)
+
+    many((U - 1) * 4 * T, D, qd_s.at[0])
+    many((U - 1) * 2 * T, D, kv_s.at[0])
+    stat_wait(st_s.at[0])
+
+    @pl.when(lower)
+    def _():
+        zst(0).wait_send()
+        many(4 * R, D, zq_s.at[0])
+
+    @pl.when(has_up)
+    def _():
+        zst(1).wait_send()
+        many(2 * R, D, zk_s.at[0])
+
+    @pl.when(has_dn)
+    def _():
+        for half in range(2):
+            for which in range(2):
+                give_k(half, which).wait_send()
+
+    @pl.when(mid)
+    def _():
+        for half in range(2):
+            for h in range(GROUP):
+                give_q(half, h).wait_send()
+
     for h in range(GROUP):
         keep_q(h).wait()
     for which in range(2):
         keep_kv(which).wait()
-
-    many((U - 1) * 4 * T, D, qd_s.at[0])
-    many((U - 1) * 2 * T, D, kv_s.at[0])
-    stat_wait(st_s.at[0])
-
-    @pl.when(lower)
-    def _():
-        zst(0).wait_send()
-        many(4 * R, D, zq_s.at[0])
-
-    @pl.when(has_up)
-    def _():
-        zst(1).wait_send()
-        many(2 * R, D, zk_s.at[0])
-
-    @pl.when(has_dn)
-    def _():
-        for half in range(2):
-            for which in range(2):
-                give_k(half, which).wait_send()
-
-    @pl.when(mid)
-    def _():
-        for half in range(2):
-            for h in range(GROUP):
-                give_q(half, h).wait_send()
-
     many((U - 1) * T, GD, oq_s.at[0])
     many((U - 1) * 2 * T, D, okv_s.at[0])
     many((U - 1) * T, GD, oq_r.at[0])

time: 73.2 us -> 66.1 us (0.903)
  Pallas kernels: 72.3 us -> 64.5 us
    pallas_call x1, Pallas kernels: 70.3 us -> 62.5 us  [per_device(): pl.pallas_call(functools.partial(kernel, U, B), out_shape=(jax.ShapeDtype...]
where the time goes in v3:
time: 66.1 us; the launch traced here: 65.2 us
  Pallas kernels  64.5 us (98%)
    pallas_call x1, Pallas kernels, per_device(): pl.pallas_call(functools.partial(kernel, U, B), out_shape=(jax.ShapeDtype...  62.5 us
    pallas_call x1, Pallas kernels, per_device(): pl.pallas_call(close_kernel, out_shape=tuple((jax.ShapeDtypeStruct(r.shap...  2.01 us

profile of v3, /device:TPU:7, one launch (start us, length us, event | category | flops | bytes accessed | tf_op | source)
XLA Modules:
  0.0 65.2 jit_solution(13478483339668052119)
XLA Ops:
  0.6 62.5 %shard_map.94 = (bf16[128,2048]{1,0:T(8,128)(2,1)}, bf16[128,1024]{1,0:T(8,128)(2,1)}, bf16[128,1024]{1,0:T(8,128)(2,1)}) custom-call(bf16[128,2048]{1,0:T(8,128)(2,1)} %q_hbm.1, bf16[128,2048]{1,0:T(8,128)(2,1)} %do_hbm.1, bf16[128,1024]{1,0:T(8,128)(2,1)} %k_hbm.1, bf16[128,1024]{1,0:T(8,128)(2,1)} %v_hbm.1, bf16[128,2048]{1,0:T(8,128)(2,1)} %out_hbm.1, ...), custom_call_target="tpu_custom_call" | custom-call | tf_op jit(solution)/shard_map/pallas_call | solution.py:606
  63.1 2.0 %shard_map.95 = (bf16[128,2048]{1,0:T(8,128)(2,1)}, bf16[128,1024]{1,0:T(8,128)(2,1)}, bf16[128,1024]{1,0:T(8,128)(2,1)}) custom-call(bf16[128,2048]{1,0:T(8,128)(2,1)} %get-tuple-element.6.a_in, bf16[128,1024]{1,0:T(8,128)(2,1)} %get-tuple-element.7.b_in, bf16[128,1024]{1,0:T(8,128)(2,1)} %get-tuple-element.8.c_in), custom_call_target="tpu_custom_call" | custom-call | tf_op jit(solution)/shard_map/pallas_call | solution.py:634

commit v4 on v3

--- a/solution.py
+++ b/solution.py
@@ -31,7 +31,7 @@
     aug, kaug, vaug, qT, dT, kT, vT,
     dqa, dka, dva,
     retk, retq, ink, inq, dqs, dkvs,
-    loc_sem, keep_sem, ready,
+    loc_sem, ready,
     qd_s, qd_r, kv_s, kv_r, st_s, st_r,
     zq_s, zq_r, zk_s, zk_r, zst_s, zst_r,
     rk_s, rk_r, rq_s, rq_r, oq_s, oq_r, okv_s, okv_r,
@@ -462,18 +462,6 @@
             okv_s.at[0], okv_r.at[which], dev,
         )
 
-    def keep_q(h):
-        return pltpu.make_async_copy(
-            dqs.at[rows(u), h * D:(h + 1) * D], dq_ref.at[:, cols(u * GD + h * D, D)],
-            keep_sem.at[2 + h],
-        )
-
-    def keep_kv(which):
-        ref = (dk_ref, dv_ref)[which]
-        return pltpu.make_async_copy(
-            dkvs.at[which, rows(u), :], ref.at[:, cols(u * D, D)], keep_sem.at[which]
-        )
-
     def finish_q(h):
         @pl.when(lower)
         def _():
@@ -487,7 +475,7 @@
             oq(h, to, u, at(b, to)).start()
 
         each(1, U, go)
-        keep_q(h).start()
+        dq_ref[:, cols(u * GD + h * D, D)] = dqs[rows(u), h * D:(h + 1) * D]
 
     def finish_kv(which):
         total = (dka, dva)[which]
@@ -508,7 +496,7 @@
             okv(which, to, u, at(b, to)).start()
 
         each(1, U, go)
-        keep_kv(which).start()
+        (dk_ref, dv_ref)[which][:, cols(u * D, D)] = dkvs[which, rows(u), :]
 
     @pl.when(jnp.logical_not(late))
     def _():
@@ -553,10 +541,6 @@
             for h in range(GROUP):
                 give_q(half, h).wait_send()
 
-    for h in range(GROUP):
-        keep_q(h).wait()
-    for which in range(2):
-        keep_kv(which).wait()
     many((U - 1) * T, GD, oq_s.at[0])
     many((U - 1) * 2 * T, D, okv_s.at[0])
     many((U - 1) * T, GD, oq_r.at[0])
@@ -564,25 +548,15 @@
         many((U - 1) * T, D, okv_r.at[which])
 
 
-def close_kernel(a_in, b_in, c_in, a_out, b_out, c_out, a_mid, b_mid, c_mid, in_sem, out_sem):
-    moves = []
-    for i, (src, mid, dst) in enumerate(
-        [(a_in, a_mid, a_out), (b_in, b_mid, b_out), (c_in, c_mid, c_out)]
-    ):
-        height = src.shape[0] // PIECES
-        for n in range(PIECES):
-            part = pl.ds(n * height, height)
-            moves.append((
-                pltpu.make_async_copy(src.at[part], mid.at[part], in_sem.at[i, n]),
-                pltpu.make_async_copy(mid.at[part], dst.at[part], out_sem.at[i, n]),
-            ))
-    for load, _ in moves:
-        load.start()
-    for load, store in moves:
-        load.wait()
-        store.start()
-    for _, store in moves:
-        store.wait()
+def close_kernel(a_in, b_in, c_in, a_out, b_out, c_out, sem):
+    moves = [
+        pltpu.make_async_copy(src, dst, sem.at[i])
+        for i, (src, dst) in enumerate([(a_in, a_out), (b_in, b_out), (c_in, c_out)])
+    ]
+    for move in moves:
+        move.start()
+    for move in moves:
+        move.wait()
 
 
 def per_device(uly_count, blk_count, q, k, v, out, grad, lse_parts, segment_ids):
@@ -606,12 +580,12 @@
     results = pl.pallas_call(
         functools.partial(kernel, U, B),
         out_shape=(
-            jax.ShapeDtypeStruct(q.shape, bf),
-            jax.ShapeDtypeStruct(k.shape, bf),
-            jax.ShapeDtypeStruct(v.shape, bf),
+            pltpu.VMEM(q.shape, bf),
+            pltpu.VMEM(k.shape, bf),
+            pltpu.VMEM(v.shape, bf),
         ),
         in_specs=[pl.BlockSpec(memory_space=pltpu.HBM)] * 7,
-        out_specs=tuple([pl.BlockSpec(memory_space=pltpu.HBM)] * 3),
+        out_specs=tuple([pl.BlockSpec(memory_space=pltpu.VMEM)] * 3),
         scratch_shapes=[
             vm(q.shape, bf), vm(q.shape, bf), vm(k.shape, bf), vm(v.shape, bf),
             vm(q.shape, bf), vm(parts.shape, f32), vm((1, T), jnp.int32),
@@ -624,7 +598,7 @@
             vm((2, 2, D, R // 2), bf), vm((2, GROUP, R // 2, D), bf),
             vm((2, 2, D, R // 2), bf), vm((2, GROUP, R // 2, D), bf),
             vm((R, GD), bf), vm((2, R, D), bf),
-            dma((11,)), dma((4,)), pltpu.SemaphoreType.REGULAR,
+            dma((11,)), pltpu.SemaphoreType.REGULAR,
         ] + sems,
         compiler_params=pltpu.CompilerParams(
             collective_id=0, has_side_effects=True, vmem_limit_bytes=60 << 20
@@ -634,11 +608,10 @@
     return pl.pallas_call(
         close_kernel,
         out_shape=tuple(jax.ShapeDtypeStruct(r.shape, r.dtype) for r in results),
-        in_specs=hbm,
+        in_specs=[pl.BlockSpec(memory_space=pltpu.VMEM)] * 3,
         out_specs=tuple(hbm),
-        scratch_shapes=[vm(r.shape, r.dtype) for r in results]
-        + [dma((3, PIECES)), dma((3, PIECES))],
-        compiler_params=pltpu.CompilerParams(vmem_limit_bytes=56 << 20),
+        scratch_shapes=[dma((3,))],
+        compiler_params=pltpu.CompilerParams(vmem_limit_bytes=8 << 20),
     )(*results)
 
 

time: 66.1 us -> 64.9 us (0.982)
  Pallas kernels: 64.5 us -> 63.2 us
    pallas_call x1, Pallas kernels: 2.01 us -> 0.99 us  [per_device(): pl.pallas_call(close_kernel, out_shape=tuple((jax.ShapeDtypeStruct(r.shap...]
where the time goes in v4:
time: 64.9 us; the launch traced here: 63.9 us
  Pallas kernels  63.2 us (97%)
    pallas_call x1, Pallas kernels, per_device(): pl.pallas_call(functools.partial(kernel, U, B), out_shape=(pltpu.VMEM(q.s...  62.3 us

profile of v4, /device:TPU:7, one launch (start us, length us, event | category | flops | bytes accessed | tf_op | source)
XLA Modules:
  0.0 63.9 jit_solution(9624293429913609233)
XLA Ops:
  0.6 62.3 %shard_map.94 = (bf16[128,2048]{1,0:T(8,128)(2,1)S(1)}, bf16[128,1024]{1,0:T(8,128)(2,1)S(1)}, bf16[128,1024]{1,0:T(8,128)(2,1)S(1)}) custom-call(bf16[128,2048]{1,0:T(8,128)(2,1)} %q_hbm.1, bf16[128,2048]{1,0:T(8,128)(2,1)} %do_hbm.1, bf16[128,1024]{1,0:T(8,128)(2,1)} %k_hbm.1, bf16[128,1024]{1,0:T(8,128)(2,1)} %v_hbm.1, bf16[128,2048]{1,0:T(8,128)(2,1)} %out_hbm.1, ...), custom_call_target="tpu_custom_call" | custom-call | tf_op jit(solution)/shard_map/pallas_call | solution.py:580
  62.9 1.0 %shard_map.95 = (bf16[128,2048]{1,0:T(8,128)(2,1)}, bf16[128,1024]{1,0:T(8,128)(2,1)}, bf16[128,1024]{1,0:T(8,128)(2,1)}) custom-call(bf16[128,2048]{1,0:T(8,128)(2,1)S(1)} %get-tuple-element.6.a_in, bf16[128,1024]{1,0:T(8,128)(2,1)S(1)} %get-tuple-element.7.b_in, bf16[128,1024]{1,0:T(8,128)(2,1)S(1)} %get-tuple-element.8.c_in), custom_call_target="tpu_custom_call" | custom-call | tf_op jit(solution)/shard_map/pallas_call | solution.py:608

commit v5 on v4

--- a/solution.py
+++ b/solution.py
@@ -504,6 +504,10 @@
 
     finish_kv(1)
 
+    @pl.when(late)
+    def _():
+        finish_q(0)
+
     @pl.when(jnp.logical_not(late))
     def _():
         finish_q(1)
@@ -512,8 +516,7 @@
 
     @pl.when(late)
     def _():
-        for h in range(GROUP):
-            finish_q(h)
+        finish_q(1)
 
     many((U - 1) * 4 * T, D, qd_s.at[0])
     many((U - 1) * 2 * T, D, kv_s.at[0])

time: 64.9 us -> 62.6 us (0.965); the launches traced: 63.9 us -> 62.4 us
  Pallas kernels: 63.2 us -> 61.8 us
    pallas_call x1, Pallas kernels: 62.3 us -> 60.8 us  [per_device(): pl.pallas_call(functools.partial(kernel, U, B), out_shape=(pltpu.VMEM(q.s...]
where the time goes in v5:
time: 62.6 us; the launch traced here: 62.4 us
  Pallas kernels  61.8 us (99%)
  between operations  0.64 us (1%)
    pallas_call x1, Pallas kernels, per_device(): pl.pallas_call(functools.partial(kernel, U, B), out_shape=(pltpu.VMEM(q.s...  60.8 us

profile of v5, /device:TPU:7, one launch (start us, length us, event | category | flops | bytes accessed | tf_op | source)
XLA Modules:
  0.0 62.4 jit_solution(5010526917781561835)
XLA Ops:
  0.6 60.8 %shard_map.94 = (bf16[128,2048]{1,0:T(8,128)(2,1)S(1)}, bf16[128,1024]{1,0:T(8,128)(2,1)S(1)}, bf16[128,1024]{1,0:T(8,128)(2,1)S(1)}) custom-call(bf16[128,2048]{1,0:T(8,128)(2,1)} %q_hbm.1, bf16[128,2048]{1,0:T(8,128)(2,1)} %do_hbm.1, bf16[128,1024]{1,0:T(8,128)(2,1)} %k_hbm.1, bf16[128,1024]{1,0:T(8,128)(2,1)} %v_hbm.1, bf16[128,2048]{1,0:T(8,128)(2,1)} %out_hbm.1, ...), custom_call_target="tpu_custom_call" | custom-call | tf_op jit(solution)/shard_map/pallas_call | solution.py:583
  61.4 1.0 %shard_map.95 = (bf16[128,2048]{1,0:T(8,128)(2,1)}, bf16[128,1024]{1,0:T(8,128)(2,1)}, bf16[128,1024]{1,0:T(8,128)(2,1)}) custom-call(bf16[128,2048]{1,0:T(8,128)(2,1)S(1)} %get-tuple-element.6.a_in, bf16[128,1024]{1,0:T(8,128)(2,1)S(1)} %get-tuple-element.7.b_in, bf16[128,1024]{1,0:T(8,128)(2,1)S(1)} %get-tuple-element.8.c_in), custom_call_target="tpu_custom_call" | custom-call | tf_op jit(solution)/shard_map/pallas_call | solution.py:611
